TPU v7x, 32 devices: a whole 2x2x4 slice. The times are simulated.
32 devices in a mesh: gx: 2 (over core), gy: 4 (over y, x), rep: 4 (over z).
Axes of the slice: x: 2, y: 2, z: 4, core: 2. Of those that a mesh axis runs over, the one named last changes fastest.
Arguments:
- generator: float32 [384, 384], P('gx', 'gy'), may hold values from -1.25 to 1.25
Outputs:
- propagator: float32 [384, 384], P('gx', 'gy')
All inputs are finite; a program needn't handle non-finite values.
Results may differ from a plain program's by a relative error of at most 0.0003.
Values sent between devices are 32-bit elements.
A program may use at most 64 MiB of HBM per device.

v0:
```python
import jax
import jax.numpy as jnp
from jax import lax
from jax.sharding import PartitionSpec as P

DEGREE = 8
SQUARINGS = 4


def folded(x, axis, dim, take_in, carry):
    whole = jax.tree.map(lambda part: lax.all_gather(part, axis, axis=dim, tiled=True), x)
    return take_in(carry, whole, jnp.int32(0))


def multiply(first, second):
    return jnp.dot(
        first, second, precision=lax.Precision.HIGHEST, preferred_element_type=jnp.float32
    )


def product(first, second):
    row_count, col_count = first.shape
    empty = jnp.zeros((row_count, col_count), jnp.float32)
    column = lax.all_gather(second, "gx", axis=0, tiled=True)

    def accumulate(total, piece, start):
        stripe = lax.dynamic_slice_in_dim(column, start, piece.shape[1], 0)
        return total + multiply(piece, stripe)

    return folded(first, "gy", 1, accumulate, empty)


def shards(generator):
    row_count, col_count = generator.shape
    row_ids = (
        lax.broadcasted_iota(jnp.int32, (row_count, col_count), 0)
        + lax.axis_index("gx") * row_count
    )
    col_ids = (
        lax.broadcasted_iota(jnp.int32, (row_count, col_count), 1)
        + lax.axis_index("gy") * col_count
    )
    unit_block = jnp.where(row_ids == col_ids, 1.0, 0.0).astype(jnp.float32)
    scaled = generator / 2.0**SQUARINGS
    taylor = unit_block + scaled / DEGREE
    for power in range(DEGREE - 1, 0, -1):
        taylor = unit_block + product(scaled, taylor) / power
    for square_index in range(SQUARINGS):
        taylor = product(taylor, taylor)
    return taylor


def solution(mesh):
    placed = (P("gx", "gy"),)
    return jax.shard_map(
        shards, mesh=mesh, in_specs=placed, out_specs=P("gx", "gy"), check_vma=False
    )
```

profile of v0, /device:TPU:0, one launch (start us, length us, event | category | flops | bytes accessed | tf_op | source)
XLA Modules:
  0.0 79.6 jit_solution(744850066559615669)
XLA Ops:
  0.0 1.0 %select_add_fusion = f32[192,96]{1,0:T(8,128)S(1)} fusion(f32[192,96]{1,0:T(8,128)} %param.1, s32[96]{0:T(128)S(1)} %iota_add_fusion.1, s32[192]{0:T(256)S(1)} %iota_add_fusion), kind=kLoop, calls=%fused_computation.13 | loop fusion | flops 73728 | bytes 148608 | tf_op jit(solution)/shard_map/add | solution.py:45
  1.0 2.2 %all_gather.55 = f32[384,96]{1,0:T(8,128)S(1)} all-gather(f32[192,96]{1,0:T(8,128)S(1)} %select_add_fusion), channel_id=1, replica_groups=mesh['gx'=2,'gy'=4,'rep'=4] {'gx'}, dimensions={0}, use_global_device_ids=true | all-gather | bytes 221184 | tf_op jit(solution)/shard_map/all_gather | solution.py:24
  3.4 10.9 %all_gather.54 = f32[192,384]{0,1:T(8,128)S(1)} all-gather(f32[192,96]{0,1:T(8,128)S(1)} %broadcast_multiply_fusion), channel_id=1, replica_groups=mesh['gx'=2,'gy'=4,'rep'=4] {'gy'}, dimensions={1}, use_global_device_ids=true | all-gather | bytes 368640 | tf_op jit(solution)/shard_map/all_gather | solution.py:11
  14.2 0.8 fusion.5
  15.0 1.9 %all_gather.56 = f32[384,96]{1,0:T(8,128)S(1)} all-gather(f32[192,96]{1,0:T(8,128)S(1)} %fusion.5), channel_id=1, replica_groups=mesh['gx'=2,'gy'=4,'rep'=4] {'gx'}, dimensions={0}, use_global_device_ids=true | all-gather | bytes 221184 | tf_op jit(solution)/shard_map/all_gather | solution.py:24
  17.0 0.8 fusion.4
  17.8 1.9 %all_gather.57 = f32[384,96]{1,0:T(8,128)S(1)} all-gather(f32[192,96]{1,0:T(8,128)S(1)} %fusion.4), channel_id=1, replica_groups=mesh['gx'=2,'gy'=4,'rep'=4] {'gx'}, dimensions={0}, use_global_device_ids=true | all-gather | bytes 221184 | tf_op jit(solution)/shard_map/all_gather | solution.py:24
  20.5 1.9 %all_gather.58 = f32[384,96]{1,0:T(8,128)S(1)} all-gather(f32[192,96]{1,0:T(8,128)S(1)} %fusion.3), channel_id=1, replica_groups=mesh['gx'=2,'gy'=4,'rep'=4] {'gx'}, dimensions={0}, use_global_device_ids=true | all-gather | bytes 221184 | tf_op jit(solution)/shard_map/all_gather | solution.py:24
  23.3 1.9 %all_gather.59 = f32[384,96]{1,0:T(8,128)S(1)} all-gather(f32[192,96]{1,0:T(8,128)S(1)} %fusion.2), channel_id=1, replica_groups=mesh['gx'=2,'gy'=4,'rep'=4] {'gx'}, dimensions={0}, use_global_device_ids=true | all-gather | bytes 221184 | tf_op jit(solution)/shard_map/all_gather | solution.py:24
  25.2 0.8 fusion.1
  26.0 1.9 %all_gather.60 = f32[384,96]{1,0:T(8,128)S(1)} all-gather(f32[192,96]{1,0:T(8,128)S(1)} %fusion.1), channel_id=1, replica_groups=mesh['gx'=2,'gy'=4,'rep'=4] {'gx'}, dimensions={0}, use_global_device_ids=true | all-gather | bytes 221184 | tf_op jit(solution)/shard_map/all_gather | solution.py:24
  28.8 1.9 %all_gather.61 = f32[384,96]{1,0:T(8,128)S(1)} all-gather(f32[192,96]{1,0:T(8,128)S(1)} %fusion), channel_id=1, replica_groups=mesh['gx'=2,'gy'=4,'rep'=4] {'gx'}, dimensions={0}, use_global_device_ids=true | all-gather | bytes 221184 | tf_op jit(solution)/shard_map/all_gather | solution.py:24
  31.6 1.9 %all_gather.63 = f32[384,96]{1,0:T(8,128)S(1)} all-gather(f32[192,96]{1,0:T(8,128)S(1)} %convolution_add_fusion), channel_id=1, replica_groups=mesh['gx'=2,'gy'=4,'rep'=4] {'gx'}, dimensions={0}, use_global_device_ids=true | all-gather | bytes 221184 | tf_op jit(solution)/shard_map/all_gather | solution.py:24
  33.6 9.5 %all_gather.62 = f32[192,384]{0,1:T(8,128)S(1)} all-gather(f32[192,96]{0,1:T(8,128)S(1)} %copy.3), channel_id=1, replica_groups=mesh['gx'=2,'gy'=4,'rep'=4] {'gy'}, dimensions={1}, use_global_device_ids=true | all-gather | bytes 368640 | tf_op jit(solution)/shard_map/all_gather | solution.py:11
  43.1 0.8 %fusion.6 = f32[192,96]{1,0:T(8,128)S(1)} fusion(f32[192,384]{0,1:T(8,128)S(1)} %all_gather.62, f32[384,96]{1,0:T(8,128)S(1)} %all_gather.63), kind=kOutput, calls=%fused_computation.17 | convolution fusion | flops 84934656 | bytes 516096 | tf_op jit(solution)/shard_map/dot_general | solution.py:16
  44.0 1.9 %all_gather.65 = f32[384,96]{1,0:T(8,128)S(1)} all-gather(f32[192,96]{1,0:T(8,128)S(1)} %fusion.6), channel_id=1, replica_groups=mesh['gx'=2,'gy'=4,'rep'=4] {'gx'}, dimensions={0}, use_global_device_ids=true | all-gather | bytes 221184 | tf_op jit(solution)/shard_map/all_gather | solution.py:24
  45.9 8.5 %all_gather.64 = f32[192,384]{0,1:T(8,128)S(1)} all-gather(f32[192,96]{0,1:T(8,128)S(1)} %copy.4), channel_id=1, replica_groups=mesh['gx'=2,'gy'=4,'rep'=4] {'gy'}, dimensions={1}, use_global_device_ids=true | all-gather | bytes 368640 | tf_op jit(solution)/shard_map/all_gather | solution.py:11
  54.4 0.8 fusion.7
  55.3 1.9 %all_gather.67 = f32[384,96]{1,0:T(8,128)S(1)} all-gather(f32[192,96]{1,0:T(8,128)S(1)} %fusion.7), channel_id=1, replica_groups=mesh['gx'=2,'gy'=4,'rep'=4] {'gx'}, dimensions={0}, use_global_device_ids=true | all-gather | bytes 221184 | tf_op jit(solution)/shard_map/all_gather | solution.py:24
  57.3 9.5 %all_gather.66 = f32[192,384]{0,1:T(8,128)S(1)} all-gather(f32[192,96]{0,1:T(8,128)S(1)} %copy.5), channel_id=1, replica_groups=mesh['gx'=2,'gy'=4,'rep'=4] {'gy'}, dimensions={1}, use_global_device_ids=true | all-gather | bytes 368640 | tf_op jit(solution)/shard_map/all_gather | solution.py:11
  66.8 0.8 fusion.8
  67.7 1.9 %all_gather.69 = f32[384,96]{1,0:T(8,128)S(1)} all-gather(f32[192,96]{1,0:T(8,128)S(1)} %fusion.8), channel_id=1, replica_groups=mesh['gx'=2,'gy'=4,'rep'=4] {'gx'}, dimensions={0}, use_global_device_ids=true | all-gather | bytes 221184 | tf_op jit(solution)/shard_map/all_gather | solution.py:24
  69.6 8.5 %all_gather.68 = f32[192,384]{0,1:T(8,128)S(1)} all-gather(f32[192,96]{0,1:T(8,128)S(1)} %copy.6), channel_id=1, replica_groups=mesh['gx'=2,'gy'=4,'rep'=4] {'gy'}, dimensions={1}, use_global_device_ids=true | all-gather | bytes 368640 | tf_op jit(solution)/shard_map/all_gather | solution.py:11
  78.2 1.4 %fusion.9 = f32[192,96]{1,0:T(8,128)} fusion(f32[192,384]{0,1:T(8,128)S(1)} %all_gather.68, f32[384,96]{1,0:T(8,128)S(1)} %all_gather.69), kind=kOutput, calls=%fused_computation.20 | convolution fusion | flops 84934656 | bytes 516096 | tf_op jit(solution)/shard_map/dot_general | solution.py:16
  (14 shorter events, 3.6 us)
Async XLA Ops:
  1.0 2.3 %copy-start = (f32[192,96]{1,0:T(8,128)S(1)}, f32[192,96]{1,0:T(8,128)}, u32[]{:S(2)}) copy-start(f32[192,96]{1,0:T(8,128)} %param.1) | copy-start | bytes 221188
where the time goes:
time: 79.9 us; the launch traced here: 79.6 us
  blocking collectives  68.6 us (86%)
  matrix products  9.38 us (12%)
  other arithmetic  1 us (1%)
    all_gather x5, blocking collectives, folded(): lax.all_gather(part, axis, axis=dim, tiled=True)  46.9 us
    all_gather x11, blocking collectives, product(): column = lax.all_gather(second, 'gx', axis=0, tiled=True)  21.7 us
    dot_general x11, matrix products, multiply(): jnp.dot(first, second, precision=lax.Precision.HIGHEST, preferred_element...  9.38 us

commit v1 on v0

v1 whole, which is shorter than its diff:
```python
import functools
import math

import jax
import jax.numpy as jnp
from jax import lax
from jax.experimental import pallas as pl
from jax.experimental.pallas import tpu as pltpu
from jax.sharding import PartitionSpec as P

DEGREE = 8
SQUARINGS = 4
CHUNKS = 2
VMEM_BUDGET = 40 * 2**20

ROOT = math.sqrt(177.0)
X3 = 2.0 / 3.0
X1 = X3 * (1.0 + ROOT) / 88.0
X2 = X3 * (1.0 + ROOT) / 352.0
X4 = (-271.0 + 29.0 * ROOT) / (315.0 * X3)
X5 = 11.0 * (-1.0 + ROOT) / (1260.0 * X3)
X6 = 11.0 * (-9.0 + ROOT) / (5040.0 * X3)
X7 = (89.0 - ROOT) / (5040.0 * X3 * X3)
Y2 = (857.0 - 58.0 * ROOT) / 630.0


def split(x):
    high = x.astype(jnp.bfloat16)
    return high, (x - high.astype(jnp.float32)).astype(jnp.bfloat16)


def times(x, y):
    dot = functools.partial(jnp.dot, preferred_element_type=jnp.float32)
    return dot(x[0], y[0]) + (dot(x[0], y[1]) + dot(x[1], y[0]))


def flipped(index, mask):
    bit = 1
    while bit <= mask:
        if mask & bit:
            index = index + (1 - 2 * ((index // bit) % 2)) * bit
        bit *= 2
    return index


def whole_kernel(nx, ny, gen, out, parts, th, tl, send, land, relay, relayed, own):
    rows, cols = out.shape
    order = ny * cols
    span = rows // CHUNKS
    gx, gy = lax.axis_index("gx"), lax.axis_index("gy")

    barrier = pltpu.get_barrier_semaphore()
    for mask in range(1, ny):
        pl.semaphore_signal(barrier, inc=1, device_id={"gy": flipped(gy, mask)})
    for dx in range(1, nx):
        pl.semaphore_signal(barrier, inc=1, device_id={"gx": (gx + dx) % nx})
    mine = pltpu.make_async_copy(gen, parts.at[gx, 0], own)
    mine.start()
    pl.semaphore_wait(barrier, ny + nx - 2)

    out_copies, in_copies, passed = [], [], []

    def pass_on(mask, c, src):
        piece = pl.ds(c * span, span)
        for dx in range(1, nx):
            copy = pltpu.make_async_remote_copy(
                src, parts.at[gx, mask, piece, :],
                relay.at[dx - 1, mask, c], relayed.at[dx - 1, mask, c],
                device_id={"gx": (gx + dx) % nx},
            )
            copy.start()
            passed.append(copy)

    for c in range(CHUNKS):
        piece = pl.ds(c * span, span)
        for mask in range(ny - 1, 0, -1):
            copy = pltpu.make_async_remote_copy(
                gen.at[piece, :], parts.at[gx, mask, piece, :],
                send.at[mask, c], land.at[mask, c],
                device_id={"gy": flipped(gy, mask)},
            )
            copy.start()
            out_copies.append(copy)
    for c in range(CHUNKS):
        pass_on(0, c, gen.at[pl.ds(c * span, span), :])
    for c in range(CHUNKS):
        for mask in range(1, ny):
            piece = pl.ds(c * span, span)
            out_copies[c * (ny - 1) + ny - 1 - mask].wait_recv()
            pass_on(mask, c, parts.at[gx, mask, piece, :])
    mine.wait()
    for copy in passed:
        copy.wait_recv()

    per = rows // cols
    bands = []
    for p in range(ny):
        block = flipped(gy, p)
        x_of, at = block // per, pl.multiple_of((block % per) * cols, cols)
        bands.append(
            jnp.concatenate([parts[x_of, m, pl.ds(at, cols), :] for m in range(ny)], axis=1)
        )
    a = jnp.concatenate(bands, axis=0) * (1.0 / 2.0**SQUARINGS)
    unit = jnp.where(
        lax.broadcasted_iota(jnp.int32, (order, order), 0)
        == lax.broadcasted_iota(jnp.int32, (order, order), 1),
        1.0, 0.0,
    )
    a_s = split(a)
    a2 = times(a_s, a_s)
    a4 = times(split(a2), split(X1 * a + X2 * a2))
    left = X3 * a2 + a4
    right = X5 * a + X6 * a2 + X7 * a4
    t = times(split(left), split(right)) + (unit + a + Y2 * a2 + X4 * left)
    for _ in range(SQUARINGS - 2):
        t_s = split(t)
        t = times(t_s, t_s)
    th[...], tl[...] = split(t)
    row_h, row_l = [], []
    for r in range(per):
        block = gx * per + r
        at, bit = 0, 1
        while bit < ny:
            at = at + ((block // bit + gy // bit) % 2) * bit
            bit *= 2
        at = pl.ds(pl.multiple_of(at * cols, cols), cols)
        row_h.append(th[at, :])
        row_l.append(tl[at, :])
    band = (jnp.concatenate(row_h, axis=0), jnp.concatenate(row_l, axis=0))
    full = (th[...], tl[...])
    column = (th[:, :cols], tl[:, :cols])
    out[...] = times(split(times(band, full)), split(times(full, column)))

    for copy in out_copies:
        copy.wait_send()
    for copy in passed:
        copy.wait_send()


def whole_on_each(nx, ny, generator):
    rows, cols = generator.shape
    order = ny * cols
    dma = pltpu.SemaphoreType.DMA
    return pl.pallas_call(
        functools.partial(whole_kernel, nx, ny),
        out_shape=jax.ShapeDtypeStruct((rows, cols), jnp.float32),
        in_specs=[pl.BlockSpec(memory_space=pl.ANY)],
        out_specs=pl.BlockSpec(memory_space=pltpu.VMEM),
        scratch_shapes=[
            pltpu.VMEM((nx, ny, rows, cols), jnp.float32),
            pltpu.VMEM((order, order), jnp.bfloat16),
            pltpu.VMEM((order, order), jnp.bfloat16),
            dma((ny, CHUNKS)),
            dma((ny, CHUNKS)),
            dma((nx - 1, ny, CHUNKS)),
            dma((nx - 1, ny, CHUNKS)),
            dma,
        ],
        compiler_params=pltpu.CompilerParams(collective_id=0, has_side_effects=True),
    )(generator)


def multiply(first, second):
    return jnp.dot(
        first, second, precision=lax.Precision.HIGHEST, preferred_element_type=jnp.float32
    )


def product(first, second):
    column = lax.all_gather(second, "gx", axis=0, tiled=True)
    return multiply(lax.all_gather(first, "gy", axis=1, tiled=True), column)


def in_blocks(generator):
    rows, cols = generator.shape
    row_ids = lax.broadcasted_iota(jnp.int32, (rows, cols), 0) + lax.axis_index("gx") * rows
    col_ids = lax.broadcasted_iota(jnp.int32, (rows, cols), 1) + lax.axis_index("gy") * cols
    unit = jnp.where(row_ids == col_ids, 1.0, 0.0).astype(jnp.float32)
    a = generator / 2.0**SQUARINGS
    a2 = product(a, a)
    a4 = product(a2, X1 * a + X2 * a2)
    left = X3 * a2 + a4
    t = product(left, X5 * a + X6 * a2 + X7 * a4) + (unit + a + Y2 * a2 + X4 * left)
    for _ in range(SQUARINGS):
        t = product(t, t)
    return t


def solution(mesh):
    nx, ny = mesh.shape["gx"], mesh.shape["gy"]

    def shards(generator):
        rows, cols = generator.shape
        fits = 12 * 4 * (nx * rows) * (ny * cols) <= VMEM_BUDGET
        square = nx * rows == ny * cols and rows % cols == 0
        if fits and square and ny & (ny - 1) == 0 and rows % (8 * CHUNKS) == 0 and cols % 16 == 0:
            return whole_on_each(nx, ny, generator)
        return in_blocks(generator)

    return jax.shard_map(
        shards, mesh=mesh, in_specs=(P("gx", "gy"),), out_specs=P("gx", "gy"), check_vma=False
    )
```

time: 79.9 us -> 17.7 us (0.22)
  the two profiles are of different devices: /device:TPU:0 before, /device:TPU:1 now
where the time goes in v1:
time: 17.7 us; the launch traced here: 17.6 us
  Pallas kernels  16 us (90%)
  local copies, waits for them, and re-layouts  1.54 us (9%)
    pallas_call x1, Pallas kernels, whole_on_each(): pl.pallas_call(functools.partial(whole_kernel, nx, ny), out_shape=jax.Sha...  16 us
    unnamed x1, local copies, waits for them, and re-layouts  1.54 us

profile of v1, /device:TPU:1, one launch (start us, length us, event | category | flops | bytes accessed | tf_op | source)
XLA Modules:
  0.0 17.6 jit_solution(18407367423474792914)
XLA Ops:
  0.0 16.0 %shard_map.17 = f32[192,96]{1,0:T(8,128)} custom-call(f32[192,96]{1,0:T(8,128)} %gen.1), custom_call_target="tpu_custom_call" | custom-call | tf_op jit(solution)/shard_map/pallas_call | solution.py:144
  16.0 1.5 %copy.3 = f32[192,96]{1,0:T(8,128)} copy(f32[192,96]{1,0:T(8,128)} %shard_map.17) | data formatting | bytes 147456

commit v2 on v1

--- a/solution.py
+++ b/solution.py
@@ -11,6 +11,8 @@
 DEGREE = 8
 SQUARINGS = 4
 CHUNKS = 2
+LANES = 128
+MATMUL = 256
 VMEM_BUDGET = 40 * 2**20
 
 ROOT = math.sqrt(177.0)
@@ -31,7 +33,27 @@
 
 def times(x, y):
     dot = functools.partial(jnp.dot, preferred_element_type=jnp.float32)
-    return dot(x[0], y[0]) + (dot(x[0], y[1]) + dot(x[1], y[0]))
+    both = jnp.concatenate(x, axis=1)
+    width = y[0].shape[1]
+    whole = width // MATMUL * MATMUL
+    if width - whole > MATMUL // 2:
+        whole = width
+    done = []
+    if whole:
+        high, low = y[0][:, :whole], y[1][:, :whole]
+        done.append(dot(both, jnp.concatenate([high, high], axis=0)) + dot(x[0], low))
+    if whole < width:
+        high, low = y[0][:, whole:], y[1][:, whole:]
+        pair = jnp.concatenate(
+            [
+                jnp.concatenate([high, low], axis=1),
+                jnp.concatenate([high, jnp.zeros_like(low)], axis=1),
+            ],
+            axis=0,
+        )
+        two = dot(both, pair)
+        done.append(two[:, : width - whole] + two[:, width - whole :])
+    return done[0] if len(done) == 1 else jnp.concatenate(done, axis=1)
 
 
 def flipped(index, mask):
@@ -43,29 +65,46 @@
     return index
 
 
-def whole_kernel(nx, ny, gen, out, parts, th, tl, send, land, relay, relayed, own):
+def packed(x):
+    cols = x.shape[1]
+    free = LANES - cols
+    tail = x.shape[0] * free // LANES
+    body = x.shape[0] - tail
+    side = jnp.concatenate([x[body:, k : k + free] for k in range(0, cols, free)], axis=0)
+    return jnp.concatenate([x[:body], side], axis=1)
+
+
+def unpacked(x, cols):
+    tail = x.shape[0] * (LANES - cols) // cols
+    side = [x[k : k + tail, cols:] for k in range(0, x.shape[0], tail)]
+    return jnp.concatenate([x[:, :cols], jnp.concatenate(side, axis=1)], axis=0)
+
+
+def whole_kernel(nx, ny, gen, out, local, parts, af, th, tl, send, land, relay, relayed, own):
     rows, cols = out.shape
     order = ny * cols
-    span = rows // CHUNKS
+    per = rows // cols
+    span = parts.shape[2] // CHUNKS
     gx, gy = lax.axis_index("gx"), lax.axis_index("gy")
 
     barrier = pltpu.get_barrier_semaphore()
+    mine = pltpu.make_async_copy(gen, local, own)
+    mine.start()
     for mask in range(1, ny):
         pl.semaphore_signal(barrier, inc=1, device_id={"gy": flipped(gy, mask)})
     for dx in range(1, nx):
         pl.semaphore_signal(barrier, inc=1, device_id={"gx": (gx + dx) % nx})
-    mine = pltpu.make_async_copy(gen, parts.at[gx, 0], own)
-    mine.start()
+    mine.wait()
+    parts[gx, 0] = packed(local[...])
     pl.semaphore_wait(barrier, ny + nx - 2)
 
-    out_copies, in_copies, passed = [], [], []
-
-    def pass_on(mask, c, src):
-        piece = pl.ds(c * span, span)
+    out_copies, passed = [], []
+
+    def pass_on(mask, c):
+        piece = parts.at[gx, mask, pl.ds(c * span, span), :]
         for dx in range(1, nx):
             copy = pltpu.make_async_remote_copy(
-                src, parts.at[gx, mask, piece, :],
-                relay.at[dx - 1, mask, c], relayed.at[dx - 1, mask, c],
+                piece, piece, relay.at[dx - 1, mask, c], relayed.at[dx - 1, mask, c],
                 device_id={"gx": (gx + dx) % nx},
             )
             copy.start()
@@ -75,32 +114,34 @@
         piece = pl.ds(c * span, span)
         for mask in range(ny - 1, 0, -1):
             copy = pltpu.make_async_remote_copy(
-                gen.at[piece, :], parts.at[gx, mask, piece, :],
+                parts.at[gx, 0, piece, :], parts.at[gx, mask, piece, :],
                 send.at[mask, c], land.at[mask, c],
                 device_id={"gy": flipped(gy, mask)},
             )
             copy.start()
             out_copies.append(copy)
     for c in range(CHUNKS):
-        pass_on(0, c, gen.at[pl.ds(c * span, span), :])
+        pass_on(0, c)
     for c in range(CHUNKS):
         for mask in range(1, ny):
-            piece = pl.ds(c * span, span)
             out_copies[c * (ny - 1) + ny - 1 - mask].wait_recv()
-            pass_on(mask, c, parts.at[gx, mask, piece, :])
-    mine.wait()
+            pass_on(mask, c)
     for copy in passed:
         copy.wait_recv()
 
-    per = rows // cols
-    bands = []
-    for p in range(ny):
-        block = flipped(gy, p)
-        x_of, at = block // per, pl.multiple_of((block % per) * cols, cols)
-        bands.append(
-            jnp.concatenate([parts[x_of, m, pl.ds(at, cols), :] for m in range(ny)], axis=1)
-        )
-    a = jnp.concatenate(bands, axis=0) * (1.0 / 2.0**SQUARINGS)
+    def place(block):
+        at, bit = 0, 1
+        while bit < ny:
+            at = at + ((block // bit + gy // bit) % 2) * bit
+            bit *= 2
+        return pl.ds(pl.multiple_of(at * cols, cols), cols)
+
+    for x in range(nx):
+        band = jnp.concatenate([unpacked(parts[x, m], cols) for m in range(ny)], axis=1)
+        band = band * (1.0 / 2.0**SQUARINGS)
+        for r in range(per):
+            af[place(x * per + r), :] = band[r * cols : (r + 1) * cols]
+    a = af[...]
     unit = jnp.where(
         lax.broadcasted_iota(jnp.int32, (order, order), 0)
         == lax.broadcasted_iota(jnp.int32, (order, order), 1),
@@ -116,20 +157,11 @@
         t_s = split(t)
         t = times(t_s, t_s)
     th[...], tl[...] = split(t)
-    row_h, row_l = [], []
-    for r in range(per):
-        block = gx * per + r
-        at, bit = 0, 1
-        while bit < ny:
-            at = at + ((block // bit + gy // bit) % 2) * bit
-            bit *= 2
-        at = pl.ds(pl.multiple_of(at * cols, cols), cols)
-        row_h.append(th[at, :])
-        row_l.append(tl[at, :])
-    band = (jnp.concatenate(row_h, axis=0), jnp.concatenate(row_l, axis=0))
+    rows_at = [place(gx * per + r) for r in range(per)]
+    band = tuple(jnp.concatenate([t[at, :] for at in rows_at], axis=0) for t in (th, tl))
     full = (th[...], tl[...])
-    column = (th[:, :cols], tl[:, :cols])
-    out[...] = times(split(times(band, full)), split(times(full, column)))
+    column = (th[:, :LANES], tl[:, :LANES])
+    out[...] = times(split(times(band, full)), split(times(full, column)))[:, :cols]
 
     for copy in out_copies:
         copy.wait_send()
@@ -147,7 +179,9 @@
         in_specs=[pl.BlockSpec(memory_space=pl.ANY)],
         out_specs=pl.BlockSpec(memory_space=pltpu.VMEM),
         scratch_shapes=[
-            pltpu.VMEM((nx, ny, rows, cols), jnp.float32),
+            pltpu.VMEM((rows, cols), jnp.float32),
+            pltpu.VMEM((nx, ny, rows * cols // LANES, LANES), jnp.float32),
+            pltpu.VMEM((order, order), jnp.float32),
             pltpu.VMEM((order, order), jnp.bfloat16),
             pltpu.VMEM((order, order), jnp.bfloat16),
             dma((ny, CHUNKS)),
@@ -193,7 +227,10 @@
         rows, cols = generator.shape
         fits = 12 * 4 * (nx * rows) * (ny * cols) <= VMEM_BUDGET
         square = nx * rows == ny * cols and rows % cols == 0
-        if fits and square and ny & (ny - 1) == 0 and rows % (8 * CHUNKS) == 0 and cols % 16 == 0:
+        order_of = ny * cols
+        free = LANES - cols
+        packs = free > 0 and cols % free == 0 and rows * free % (LANES * 8 * CHUNKS) == 0
+        if fits and square and ny & (ny - 1) == 0 and packs and cols % 16 == 0 and order_of % LANES == 0:
             return whole_on_each(nx, ny, generator)
         return in_blocks(generator)
 

time: 17.7 us -> 16 us (0.904)
  Pallas kernels: 16 us -> 14.3 us
    pallas_call x1, Pallas kernels: 16 us -> 14.3 us  [whole_on_each(): pl.pallas_call(functools.partial(whole_kernel, nx, ny), out_shape=jax.Sha...]
where the time goes in v2:
time: 16 us; the launch traced here: 15.8 us
  Pallas kernels  14.3 us (89%)
  local copies, waits for them, and re-layouts  1.54 us (10%)
    pallas_call x1, Pallas kernels, whole_on_each(): pl.pallas_call(functools.partial(whole_kernel, nx, ny), out_shape=jax.Sha...  14.3 us
    unnamed x1, local copies, waits for them, and re-layouts  1.54 us

profile of v2, /device:TPU:1, one launch (start us, length us, event | category | flops | bytes accessed | tf_op | source)
XLA Modules:
  0.0 15.8 jit_solution(6727580397487841113)
XLA Ops:
  0.0 14.3 %shard_map.17 = f32[192,96]{1,0:T(8,128)} custom-call(f32[192,96]{1,0:T(8,128)} %gen.1), custom_call_target="tpu_custom_call" | custom-call | tf_op jit(solution)/shard_map/pallas_call | solution.py:176
  14.3 1.5 %copy.3 = f32[192,96]{1,0:T(8,128)} copy(f32[192,96]{1,0:T(8,128)} %shard_map.17) | data formatting | bytes 147456

commit v3 on v2

--- a/solution.py
+++ b/solution.py
@@ -175,7 +175,7 @@
     dma = pltpu.SemaphoreType.DMA
     return pl.pallas_call(
         functools.partial(whole_kernel, nx, ny),
-        out_shape=jax.ShapeDtypeStruct((rows, cols), jnp.float32),
+        out_shape=pltpu.VMEM((rows, cols), jnp.float32),
         in_specs=[pl.BlockSpec(memory_space=pl.ANY)],
         out_specs=pl.BlockSpec(memory_space=pltpu.VMEM),
         scratch_shapes=[

time: 16 us -> 14.4 us (0.900)
  local copies, waits for them, and re-layouts: 1.54 us -> 0.64 us
  Pallas kernels: 14.3 us -> 13.6 us
    unnamed x1, local copies, waits for them, and re-layouts: 1.54 us -> 0.64 us
    pallas_call x1, Pallas kernels: 14.3 us -> 13.6 us  [whole_on_each(): pl.pallas_call(functools.partial(whole_kernel, nx, ny), out_shape=pltpu.V...]
where the time goes in v3:
time: 14.4 us; the launch traced here: 14.3 us
  Pallas kernels  13.6 us (94%)
  local copies, waits for them, and re-layouts  0.64 us (4%)
    pallas_call x1, Pallas kernels, whole_on_each(): pl.pallas_call(functools.partial(whole_kernel, nx, ny), out_shape=pltpu.V...  13.6 us
    unnamed x1, local copies, waits for them, and re-layouts  0.64 us

profile of v3, /device:TPU:1, one launch (start us, length us, event | category | flops | bytes accessed | tf_op | source)
XLA Modules:
  0.0 14.3 jit_solution(15044742385527958030)
XLA Ops:
  0.0 13.6 %shard_map.17 = f32[192,96]{1,0:T(8,128)S(1)} custom-call(f32[192,96]{1,0:T(8,128)} %gen.1), custom_call_target="tpu_custom_call" | custom-call | tf_op jit(solution)/shard_map/pallas_call | solution.py:176
  13.6 0.6 %copy.3 = f32[192,96]{1,0:T(8,128)} copy(f32[192,96]{1,0:T(8,128)S(1)} %shard_map.17) | data formatting | bytes 147456
